TPU v7x, 32 devices: a whole 2x2x4 slice. The times are simulated.
32 devices in a mesh: gx: 4 (over y, core), gy: 4 (over z), gz: 2 (over x).
Axes of the slice: x: 2, y: 2, z: 4, core: 2. Of those that a mesh axis runs over, the one named last changes fastest.
Arguments:
- moments: float32 [8, 16, 64, 1024], P(None, 'gx', 'gy', 'gz'), may hold values from 0.001 to 60, as said below
- velocity: float32 [3, 16, 64, 1024], P(None, 'gx', 'gy', 'gz'), may hold values from -4 to 4
- drift: float32 [3, 16, 64, 1024], P(None, 'gx', 'gy', 'gz'), may hold values from -8 to 8
Outputs:
- updated: float32 [8, 16, 64, 1024], P(None, 'gx', 'gy', 'gz')
- totals: float32 [8], replicated
Inputs may be any that keep to these rules, and one draw needn't show every extreme that they name: In every cell the 8 entries are the moments of order 0 to 7 of a log-normal distribution of particle size.
All inputs are finite; a program needn't handle non-finite values. Where the computation divides by a largest or mean magnitude, that divisor is 1e-20 or more.
Results may differ from a plain program's by a relative error of at most 0.0003.
Values sent between devices are 32-bit elements; how exact they have to be, the bound alone decides.
A program may use at most 64 MiB of HBM per device.

v0:
```python
import jax
import jax.numpy as jnp
from jax import lax
from jax.sharding import PartitionSpec as P

SWEEPS = 6
cfl_number = 0.4
speed_eps = 1e-06
pair_list = ((0, 1), (0, 2), (0, 3), (1, 2), (1, 3), (2, 3))


def padded(shard, sides, width, wrap):
    for axis, dim in sides:
        count, length = (lax.axis_size(axis), shard.shape[dim])
        up = [(i, (i + 1) % count) for i in range(count if wrap else count - 1)]
        down = [(j, i) for i, j in up]
        last = lax.slice_in_dim(shard, length - width, length, axis=dim)
        leading = lax.slice_in_dim(shard, 0, width, axis=dim)
        before = lax.ppermute(last, axis, up)
        after = lax.ppermute(leading, axis, down)
        shard = jnp.concatenate([before, shard, after], axis=dim)
    return shard


def entry_key(first_index, second_index):
    return (min(first_index, second_index), max(first_index, second_index))


def invert(moment):
    levels = [moment[order] for order in range(8)]
    zeros = jnp.zeros_like(levels[0])
    before = [zeros] * 8
    alphas = [levels[1] / levels[0]]
    betas = [levels[0]]
    for level in range(1, 4):
        fresh = [zeros] * 8
        for column in range(level, 8 - level):
            fresh[column] = (
                levels[column + 1]
                - alphas[level - 1] * levels[column]
                - betas[level - 1] * before[column]
            )
        alphas.append(fresh[level + 1] / fresh[level] - levels[level] / levels[level - 1])
        betas.append(fresh[level] / levels[level - 1])
        before, levels = (levels, fresh)
    table = {}
    for row_index in range(4):
        for col_index in range(row_index, 4):
            table[row_index, col_index] = zeros
    for row_index in range(4):
        table[row_index, row_index] = alphas[row_index]
    for row_index in range(3):
        table[row_index, row_index + 1] = jnp.sqrt(betas[row_index + 1])
    first = [jnp.ones_like(zeros), zeros, zeros, zeros]
    for _ in range(SWEEPS):
        for pivot, other in pair_list:
            coupling = table[pivot, other]
            head = table[pivot, pivot]
            tail = table[other, other]
            spread = tail - head
            orient = jnp.where(spread >= 0, 1.0, -1.0)
            tangent = (
                orient
                * 2.0
                * coupling
                / (jnp.abs(spread) + jnp.sqrt(spread * spread + 4.0 * coupling * coupling))
            )
            cosine = 1.0 / jnp.sqrt(1.0 + tangent * tangent)
            sine = tangent * cosine
            for rest in range(4):
                if rest != pivot and rest != other:
                    near = table[entry_key(rest, pivot)]
                    far = table[entry_key(rest, other)]
                    table[entry_key(rest, pivot)] = cosine * near - sine * far
                    table[entry_key(rest, other)] = sine * near + cosine * far
            table[pivot, pivot] = head - tangent * coupling
            table[other, other] = tail + tangent * coupling
            table[pivot, other] = jnp.zeros_like(coupling)
            first_p = first[pivot]
            first_q = first[other]
            first[pivot] = cosine * first_p - sine * first_q
            first[other] = sine * first_p + cosine * first_q
    weights = [moment[0] * first[node] * first[node] for node in range(4)]
    places = [table[node, node] for node in range(4)]
    return jnp.stack(weights + places)


def face_flux(extended, axis, count):

    def part(channel, start):
        return lax.slice_in_dim(extended[channel], start, start + count + 1, axis=axis - 1)

    mean_speed = 0.5 * (part(8, 0) + part(8, 1))
    mean_drift = 0.5 * (part(9, 0) + part(9, 1))
    zeros = jnp.zeros_like(mean_speed)
    accum = [zeros] * 8
    for node in range(4):
        for start, upwind in ((0, jnp.maximum), (1, jnp.minimum)):
            size = part(4 + node, start)
            carried = part(node, start) * upwind(mean_speed + mean_drift * size, 0.0)
            for order in range(8):
                accum[order] = accum[order] + carried
                carried = carried * size
    return jnp.stack(accum)


def shards(moments, velocity, drift):
    counts = moments.shape
    cells_total = (
        counts[1]
        * lax.axis_size("gx")
        * counts[2]
        * lax.axis_size("gy")
        * counts[3]
        * lax.axis_size("gz")
    )
    bottom = lax.axis_index("gz") == 0
    top = lax.axis_index("gz") == lax.axis_size("gz") - 1
    nodes = invert(moments)
    packs = [
        jnp.concatenate(
            [nodes, velocity[direction : direction + 1], drift[direction : direction + 1]], 0
        )
        for direction in range(3)
    ]
    extended_x = padded(packs[0], (("gx", 1),), 1, True)
    extended_y = padded(packs[1], (("gy", 2),), 1, True)
    extended_z = padded(packs[2], (("gz", 3),), 1, False)
    change = jnp.zeros_like(moments)
    for direction, extended in ((0, extended_x), (1, extended_y), (2, extended_z)):
        axis = direction + 1
        count = counts[axis]
        flux = face_flux(extended, axis, count)
        if direction == 2:
            face = lax.broadcasted_iota(jnp.int32, flux.shape, 3)
            wall = (face == 0) & bottom | (face == count) & top
            flux = jnp.where(wall, 0.0, flux)
        change = (
            change
            + lax.slice_in_dim(flux, 1, count + 1, axis=axis)
            - lax.slice_in_dim(flux, 0, count, axis=axis)
        )
    speed = jnp.zeros_like(moments[0])
    for direction in range(3):
        speed = speed + jnp.max(
            jnp.abs(velocity[direction][None] + drift[direction][None] * nodes[4:8]), axis=0
        )
    local_max = jnp.max(speed)
    global_max = lax.pmax(local_max, ("gx", "gy", "gz"))
    step_size = cfl_number / (global_max + speed_eps)
    updated = moments - step_size * change
    sums = lax.psum(jnp.sum(updated, axis=(1, 2, 3)), ("gx", "gy", "gz"))
    totals = sums / cells_total
    return (updated, totals)


def solution(mesh):
    in_specs = (P(None, "gx", "gy", "gz"), P(None, "gx", "gy", "gz"), P(None, "gx", "gy", "gz"))
    out_specs = (P(None, "gx", "gy", "gz"), P())
    return jax.shard_map(shards, mesh=mesh, in_specs=in_specs, out_specs=out_specs, check_vma=False)
```

profile of v0, /device:TPU:10, one launch (start us, length us, event | category | flops | bytes accessed | tf_op | source)
XLA Modules:
  0.0 132.4 jit_solution(10353812203924966196)
XLA Ops:
  0.6 1.1 subtract_subtract_fusion.4
  1.8 1.5 %divide_sqrt_fusion = (f32[1,4,16,512]{3,2,1,0:T(8,128)S(1)}, f32[1,4,16,512]{3,2,1,0:T(8,128)S(1)}, f32[1,4,16,512]{3,2,1,0:T(8,128)S(1)}, f32[1,4,16,512]{3,2,...) fusion(f32[8,4,16,512]{3,2,1,0:T(8,128)} %param.3, ...), kind=kLoop, calls=%fused_computation.610 | loop fusion | flops 1179648 | bytes 2228224 | tf_op jit(solution)/shard_map/sqrt | solution.py:53
  3.5 1.1 multiply_add_fusion.28
  5.5 0.9 multiply_add_fusion.23
  7.1 1.1 multiply_add_fusion.16
  8.2 0.8 multiply_subtract_fusion.105
  9.2 0.8 multiply_add_fusion.11
  10.3 0.8 multiply_add_fusion.44
  11.1 1.1 multiply_add_fusion.36
  12.8 0.6 multiply_multiply_fusion
  13.8 0.7 constant_dynamic-update-slice_fusion.18
  14.4 0.7 constant_dynamic-update-slice_fusion.17
  15.5 0.8 copy-done.4
  16.4 0.7 slice_bitcast_fusion.25
  17.4 0.8 slice_bitcast_fusion.24
  18.2 0.9 fusion.284
  19.1 1.7 %collective-permute-start.1 = (f32[10,1,16,512]{3,2,1,0:T(8,128)}, f32[10,1,16,512]{3,2,1,0:T(8,128)S(1)}, u32[]{:S(2)}, u32[]{:S(2)}) collective-permute-start(f32[10,1,16,512]{3,2,1,0:T(8,128)} %get-tuple-element.278), channel_id=1, source_target_pairs={{8,0},{16,8},{24,16},{0,24},{9,1},{17,9},{25,17},{1,25},{10,2},{18... | collective-permute-start | bytes 983048 | tf_op jit(solution)/shard_map/ppermute | solution.py:20
  20.9 0.8 fusion.285
  21.6 0.7 copy.31
  22.3 1.6 %collective-permute-start.2 = (f32[10,4,1,512]{3,0,2,1:T(8,128)}, f32[10,4,1,512]{3,0,2,1:T(8,128)}, u32[]{:S(2)}, u32[]{:S(2)}) collective-permute-start(f32[10,4,1,512]{3,0,2,1:T(8,128)} %copy.31), channel_id=1, source_target_pairs={{0,2},{2,4},{4,6},{6,0},{1,3},{3,5},{5,7},{7,1},{8,10},{10,12},{12... | collective-permute-start | bytes 245768 | tf_op jit(solution)/shard_map/ppermute | solution.py:19
  23.9 0.9 fusion.286
  24.9 1.3 collective-permute-start.4
  26.1 6.0 %collective-permute-start.5 = (f32[10,4,16,1]{3,2,1,0:T(8,128)}, f32[10,4,16,1]{3,2,1,0:T(8,128)}, u32[]{:S(2)}, u32[]{:S(2)}) collective-permute-start(f32[10,4,16,1]{3,2,1,0:T(8,128)} %get-tuple-element.282), channel_id=1, source_target_pairs={{1,0},{3,2},{5,4},{7,6},{9,8},{11,10},{13,12},{15,14},{17,16},{19,... | collective-permute-start | bytes 7688 | tf_op jit(solution)/shard_map/ppermute | solution.py:20
  32.1 1.4 %abs_reduce_fusion.1 = (f32[4,16,512]{2,1,0:T(8,128)S(1)}, f32[4,16,512]{2,1,0:T(8,128)S(1)}, f32[4,16,512]{2,1,0:T(8,128)S(1)}) fusion(f32[4,16,512]{2,1,0:T(8,128)} %get-tuple-element.293, f32[4,16,512]{2,1,0:T(8,128)} %get-tuple-element.287, f32[1,4,16,512]{3,2,1,0:T(8,128)S(1)} %get-tuple-element.61, f32[1,4,16,512]{3,2,1,0:T(8,128)} %get-tuple-element.63, ...), kind=kLoop, calls=%fused_computation.48 | loop fusion | flops 1867776 | bytes 1703936 | tf_op jit(solution)/shard_map/reduce_max | solution.py:145
  33.6 0.6 add_reduce_fusion
  34.2 40.1 %pmax.7 = f32[]{:T(128)} all-reduce(f32[]{:T(128)} %add_reduce_fusion), channel_id=1, replica_groups=mesh['gx'=4,'gy'=4,'gz'=2] {'gx','gy','gz'}, use_global_device_ids=true, to_apply=%region_4.5 | all-reduce | flops 1 | bytes 8 | tf_op jit(solution)/shard_map/pmax | solution.py:149
  74.3 0.9 copy.32
  75.9 1.8 %collective-permute-start.3 = (f32[10,4,1,512]{3,0,2,1:T(8,128)S(1)}, f32[10,4,1,512]{3,0,2,1:T(8,128)S(1)}, u32[]{:S(2)}, u32[]{:S(2)}) collective-permute-start(f32[10,4,1,512]{3,0,2,1:T(8,128)S(1)} %copy.32), channel_id=1, source_target_pairs={{2,0},{4,2},{6,4},{0,6},{3,1},{5,3},{7,5},{1,7},{10,8},{12,10},{14... | collective-permute-start | bytes 245768 | tf_op jit(solution)/shard_map/ppermute | solution.py:20
  77.7 2.0 %pad_maximum_fusion.1 = f32[10,4,16,514]{3,2,1,0:T(8,128)S(1)} fusion(f32[10,4,16,1]{3,2,1,0:T(8,128)} %collective-permute-done.5, f32[10,4,16,512]{3,2,1,0:T(8,128)} %copy-done.1, f32[10,4,16,1]{3,2,1,0:T(8,128)} %collective-permute-done.4), kind=kLoop, calls=%fused_computation.37 | loop fusion | flops 657920 | bytes 2631680 | tf_op jit(solution)/shard_map/concatenate | solution.py:21
  82.4 1.1 copy.33
  89.5 1.6 %fusion.223 = (f32[8]{0:T(128)S(1)}, f32[8,4,16,512]{3,2,1,0:T(8,128)}) fusion(f32[8,4,16,512]{3,2,1,0:T(8,128)S(1)} %copy-done, f32[8,4,16,513]{3,2,1,0:T(8,128)S(1)} %broadcast_select_fusion, f32[8,4,17,512]{3,2,1,0:T(8,128)S(1)} %bitcast_dynamic-update-slice_fusion, f32[8,5,16,512]{3,2,1,0:T(8,128)S(1)} %add_dynamic-update-slice_fusion, f32[]{:T(128)S(6)} %div.553), kind=kLoop, calls=%fused_computation.747 | loop fusion | flops 2097144 | bytes 8388644 | tf_op jit(solution)/shard_map/reduce_sum | solution.py:152
  91.1 40.8 %psum.7 = f32[8]{0:T(128)S(1)} all-reduce(f32[8]{0:T(128)S(1)} %get-tuple-element.5), channel_id=1, replica_groups=mesh['gx'=4,'gy'=4,'gz'=2] {'gx','gy','gz'}, use_global_device_ids=true, to_apply=%region_6.7 | all-reduce | flops 8 | bytes 64 | tf_op jit(solution)/shard_map/psum | solution.py:152
  (70 shorter events, 12.7 us)
Async XLA Ops:
  1.8 1.7 %copy-start = (f32[8,4,16,512]{3,2,1,0:T(8,128)S(1)}, f32[8,4,16,512]{3,2,1,0:T(8,128)}, u32[]{:S(2)}) copy-start(f32[8,4,16,512]{3,2,1,0:T(8,128)} %param.3) | copy-start | bytes 3145732
  15.4 1.0 copy-start.4
  16.4 1.0 copy-start.5
  18.2 5.8 %copy-start.1 = (f32[10,4,16,512]{3,2,1,0:T(8,128)}, f32[10,4,16,512]{3,2,1,0:T(8,128)S(1)}, u32[]{:S(2)}) copy-start(f32[10,4,16,512]{3,2,1,0:T(8,128)S(1)} %get-tuple-element.291) | copy-start | bytes 3932164
  18.2 6.7 %copy-start.2 = (f32[10,4,16,512]{3,2,1,0:T(8,128)}, f32[10,4,16,512]{3,2,1,0:T(8,128)S(1)}, u32[]{:S(2)}) copy-start(f32[10,4,16,512]{3,2,1,0:T(8,128)S(1)} %get-tuple-element.290) | copy-start | bytes 3932164
  19.1 67.7 %collective-permute-start = (f32[10,1,16,512]{3,2,1,0:T(8,128)}, f32[10,1,16,512]{3,2,1,0:T(8,128)S(1)}, u32[]{:S(2)}, u32[]{:S(2)}) collective-permute-start(f32[10,1,16,512]{3,2,1,0:T(8,128)} %get-tuple-element.277), channel_id=1, source_target_pairs={{0,8},{8,16},{16,24},{24,0},{1,9},{9,17},{17,25},{25,1},{2,10},{10... | collective-permute-start | bytes 983048 | tf_op jit(solution)/shard_map/ppermute | solution.py:19
  19.1 67.7 %collective-permute-start.1 = (f32[10,1,16,512]{3,2,1,0:T(8,128)}, f32[10,1,16,512]{3,2,1,0:T(8,128)S(1)}, u32[]{:S(2)}, u32[]{:S(2)}) collective-permute-start(f32[10,1,16,512]{3,2,1,0:T(8,128)} %get-tuple-element.278), channel_id=1, source_target_pairs={{8,0},{16,8},{24,16},{0,24},{9,1},{17,9},{25,17},{1,25},{10,2},{18... | collective-permute-start | bytes 983048 | tf_op jit(solution)/shard_map/ppermute | solution.py:20
  22.3 60.0 %collective-permute-start.2 = (f32[10,4,1,512]{3,0,2,1:T(8,128)}, f32[10,4,1,512]{3,0,2,1:T(8,128)}, u32[]{:S(2)}, u32[]{:S(2)}) collective-permute-start(f32[10,4,1,512]{3,0,2,1:T(8,128)} %copy.31), channel_id=1, source_target_pairs={{0,2},{2,4},{4,6},{6,0},{1,3},{3,5},{5,7},{7,1},{8,10},{10,12},{12... | collective-permute-start | bytes 245768 | tf_op jit(solution)/shard_map/ppermute | solution.py:19
  24.9 51.0 %collective-permute-start.4 = (f32[10,4,16,1]{3,2,1,0:T(8,128)}, f32[10,4,16,1]{3,2,1,0:T(8,128)}, u32[]{:S(2)}, u32[]{:S(2)}) collective-permute-start(f32[10,4,16,1]{3,2,1,0:T(8,128)} %get-tuple-element.281), channel_id=1, source_target_pairs={{0,1},{2,3},{4,5},{6,7},{8,9},{10,11},{12,13},{14,15},{16,17},{18,... | collective-permute-start | bytes 7688 | tf_op jit(solution)/shard_map/ppermute | solution.py:19
  26.1 51.6 %collective-permute-start.5 = (f32[10,4,16,1]{3,2,1,0:T(8,128)}, f32[10,4,16,1]{3,2,1,0:T(8,128)}, u32[]{:S(2)}, u32[]{:S(2)}) collective-permute-start(f32[10,4,16,1]{3,2,1,0:T(8,128)} %get-tuple-element.282), channel_id=1, source_target_pairs={{1,0},{3,2},{5,4},{7,6},{9,8},{11,10},{13,12},{15,14},{17,16},{19,... | collective-permute-start | bytes 7688 | tf_op jit(solution)/shard_map/ppermute | solution.py:20
  75.9 7.6 %collective-permute-start.3 = (f32[10,4,1,512]{3,0,2,1:T(8,128)S(1)}, f32[10,4,1,512]{3,0,2,1:T(8,128)S(1)}, u32[]{:S(2)}, u32[]{:S(2)}) collective-permute-start(f32[10,4,1,512]{3,0,2,1:T(8,128)S(1)} %copy.32), channel_id=1, source_target_pairs={{2,0},{4,2},{6,4},{0,6},{3,1},{5,3},{7,5},{1,7},{10,8},{12,10},{14... | collective-permute-start | bytes 245768 | tf_op jit(solution)/shard_map/ppermute | solution.py:20
  82.2 1.4 %copy-start.3 = (f32[10,4,16,512]{3,2,1,0:T(8,128)S(1)}, f32[10,4,16,512]{3,2,1,0:T(8,128)}, u32[]{:S(2)}) copy-start(f32[10,4,16,512]{3,2,1,0:T(8,128)} %copy-done.2) | copy-start | bytes 3932164
where the time goes:
time: 133 us; the launch traced here: 132 us
  blocking collectives  80.9 us (61%)
  other arithmetic  28.5 us (21%)
  starting transfers between devices  12.4 us (9%)
  local copies, waits for them, and re-layouts  8.81 us (7%)
  between operations  1.78 us (1%)
    psum x1, blocking collectives, shards(): sums = lax.psum(jnp.sum(updated, axis=(1, 2, 3)), ('gx', 'gy', 'gz'))  40.8 us
    pmax x1, blocking collectives, shards(): global_max = lax.pmax(local_max, ('gx', 'gy', 'gz'))  40.1 us
    ppermute x3, starting transfers between devices, padded(): after = lax.ppermute(leading, axis, down)  9.56 us
    unnamed x25, other arithmetic  7.93 us
    add x5, other arithmetic, invert(): first[other] = sine * first_p + cosine * first_q  4.27 us
    slice x4, local copies, waits for them, and re-layouts, padded(): last = lax.slice_in_dim(shard, length - width, length, axis=dim)  3.34 us
    ppermute x3, starting transfers between devices, padded(): before = lax.ppermute(last, axis, up)  2.86 us
    add x5, other arithmetic, invert(): table[entry_key(rest, other)] = sine * near + cosine * far  2.86 us
  transfers between devices with their start and end apart: 6, of which 0 were waited for; matrix products, arithmetic and copies ran while one was open for 11% of the time, Pallas kernels for 0%

commit v1 on v0

--- a/solution.py
+++ b/solution.py
@@ -149,7 +149,8 @@
     global_max = lax.pmax(local_max, ("gx", "gy", "gz"))
     step_size = cfl_number / (global_max + speed_eps)
     updated = moments - step_size * change
-    sums = lax.psum(jnp.sum(updated, axis=(1, 2, 3)), ("gx", "gy", "gz"))
+    mat = jnp.sum(updated, axis=(1, 2, 3))
+    sums = jnp.sum(lax.all_gather(mat, ("gx", "gy", "gz")), 0)
     totals = sums / cells_total
     return (updated, totals)
 

time: 133 us -> 133 us (level)
    unnamed x0 -> x1, blocking collectives: none -> 40.9 us
    psum x1 -> x0, blocking collectives: 40.8 us -> none  [shards(): sums = lax.psum(jnp.sum(updated, axis=(1, 2, 3)), ('gx', 'gy', 'gz'))]
where the time goes in v1:
time: 133 us
  blocking collectives  80.9 us (61%)
  other arithmetic  28.6 us (22%)
  starting transfers between devices  12.4 us (9%)
  local copies, waits for them, and re-layouts  9.06 us (7%)
  between operations  1.8 us (1%)
    unnamed x1, blocking collectives  40.9 us
    pmax x1, blocking collectives, shards(): global_max = lax.pmax(local_max, ('gx', 'gy', 'gz'))  40.1 us
    ppermute x3, starting transfers between devices, padded(): after = lax.ppermute(leading, axis, down)  9.55 us
    unnamed x25, other arithmetic  8 us
    add x5, other arithmetic, invert(): first[other] = sine * first_p + cosine * first_q  4.27 us
    slice x4, local copies, waits for them, and re-layouts, padded(): last = lax.slice_in_dim(shard, length - width, length, axis=dim)  3.34 us
    ppermute x3, starting transfers between devices, padded(): before = lax.ppermute(last, axis, up)  2.86 us
    add x5, other arithmetic, invert(): table[entry_key(rest, other)] = sine * near + cosine * far  2.86 us
  transfers between devices with their start and end apart: 6, of which 0 were waited for; matrix products, arithmetic and copies ran while one was open for 11% of the time, Pallas kernels for 0%

profile of v1, /device:TPU:10, one launch (start us, length us, event | category | flops | bytes accessed | tf_op | source)
XLA Modules:
  0.0 132.8 jit_solution(7753417222536576965)
XLA Ops:
  0.6 1.1 subtract_subtract_fusion.4
  1.8 1.5 %divide_sqrt_fusion = (f32[1,4,16,512]{3,2,1,0:T(8,128)S(1)}, f32[1,4,16,512]{3,2,1,0:T(8,128)S(1)}, f32[1,4,16,512]{3,2,1,0:T(8,128)S(1)}, f32[1,4,16,512]{3,2,...) fusion(f32[8,4,16,512]{3,2,1,0:T(8,128)} %param.3, ...), kind=kLoop, calls=%fused_computation.610 | loop fusion | flops 1179648 | bytes 2228224 | tf_op jit(solution)/shard_map/sqrt | solution.py:53
  3.5 1.1 multiply_add_fusion.28
  5.5 0.9 multiply_add_fusion.23
  7.1 1.1 multiply_add_fusion.16
  8.2 0.8 multiply_subtract_fusion.105
  9.2 0.8 multiply_add_fusion.11
  10.3 0.8 multiply_add_fusion.44
  11.1 1.1 multiply_add_fusion.36
  12.8 0.6 multiply_multiply_fusion
  13.8 0.7 constant_dynamic-update-slice_fusion.18
  14.4 0.7 constant_dynamic-update-slice_fusion.17
  15.5 0.8 copy-done.4
  16.4 0.7 slice_bitcast_fusion.25
  17.4 0.8 slice_bitcast_fusion.24
  18.2 0.9 fusion.284
  19.1 1.7 %collective-permute-start.1 = (f32[10,1,16,512]{3,2,1,0:T(8,128)}, f32[10,1,16,512]{3,2,1,0:T(8,128)S(1)}, u32[]{:S(2)}, u32[]{:S(2)}) collective-permute-start(f32[10,1,16,512]{3,2,1,0:T(8,128)} %get-tuple-element.278), channel_id=1, source_target_pairs={{8,0},{16,8},{24,16},{0,24},{9,1},{17,9},{25,17},{1,25},{10,2},{18... | collective-permute-start | bytes 983048 | tf_op jit(solution)/shard_map/ppermute | solution.py:20
  20.9 0.8 fusion.285
  21.7 0.7 copy.31
  22.3 1.6 %collective-permute-start.2 = (f32[10,4,1,512]{3,0,2,1:T(8,128)}, f32[10,4,1,512]{3,0,2,1:T(8,128)}, u32[]{:S(2)}, u32[]{:S(2)}) collective-permute-start(f32[10,4,1,512]{3,0,2,1:T(8,128)} %copy.31), channel_id=1, source_target_pairs={{0,2},{2,4},{4,6},{6,0},{1,3},{3,5},{5,7},{7,1},{8,10},{10,12},{12... | collective-permute-start | bytes 245768 | tf_op jit(solution)/shard_map/ppermute | solution.py:19
  23.9 0.9 fusion.286
  24.9 1.3 collective-permute-start.4
  26.1 6.0 %collective-permute-start.5 = (f32[10,4,16,1]{3,2,1,0:T(8,128)}, f32[10,4,16,1]{3,2,1,0:T(8,128)}, u32[]{:S(2)}, u32[]{:S(2)}) collective-permute-start(f32[10,4,16,1]{3,2,1,0:T(8,128)} %get-tuple-element.282), channel_id=1, source_target_pairs={{1,0},{3,2},{5,4},{7,6},{9,8},{11,10},{13,12},{15,14},{17,16},{19,... | collective-permute-start | bytes 7688 | tf_op jit(solution)/shard_map/ppermute | solution.py:20
  32.1 1.4 %abs_reduce_fusion.1 = (f32[4,16,512]{2,1,0:T(8,128)S(1)}, f32[4,16,512]{2,1,0:T(8,128)S(1)}, f32[4,16,512]{2,1,0:T(8,128)S(1)}) fusion(f32[4,16,512]{2,1,0:T(8,128)} %get-tuple-element.293, f32[4,16,512]{2,1,0:T(8,128)} %get-tuple-element.287, f32[1,4,16,512]{3,2,1,0:T(8,128)S(1)} %get-tuple-element.61, f32[1,4,16,512]{3,2,1,0:T(8,128)} %get-tuple-element.63, ...), kind=kLoop, calls=%fused_computation.48 | loop fusion | flops 1867776 | bytes 1703936 | tf_op jit(solution)/shard_map/reduce_max | solution.py:145
  33.5 0.6 add_reduce_fusion
  34.2 40.1 %pmax.7 = f32[]{:T(128)} all-reduce(f32[]{:T(128)} %add_reduce_fusion), channel_id=1, replica_groups=mesh['gx'=4,'gy'=4,'gz'=2] {'gx','gy','gz'}, use_global_device_ids=true, to_apply=%region_4.5 | all-reduce | flops 1 | bytes 8 | tf_op jit(solution)/shard_map/pmax | solution.py:149
  74.2 0.9 copy.32
  75.9 1.8 %collective-permute-start.3 = (f32[10,4,1,512]{3,0,2,1:T(8,128)S(1)}, f32[10,4,1,512]{3,0,2,1:T(8,128)S(1)}, u32[]{:S(2)}, u32[]{:S(2)}) collective-permute-start(f32[10,4,1,512]{3,0,2,1:T(8,128)S(1)} %copy.32), channel_id=1, source_target_pairs={{2,0},{4,2},{6,4},{0,6},{3,1},{5,3},{7,5},{1,7},{10,8},{12,10},{14... | collective-permute-start | bytes 245768 | tf_op jit(solution)/shard_map/ppermute | solution.py:20
  77.7 2.0 %pad_maximum_fusion.1 = f32[10,4,16,514]{3,2,1,0:T(8,128)S(1)} fusion(f32[10,4,16,1]{3,2,1,0:T(8,128)} %collective-permute-done.5, f32[10,4,16,512]{3,2,1,0:T(8,128)} %copy-done.1, f32[10,4,16,1]{3,2,1,0:T(8,128)} %collective-permute-done.4), kind=kLoop, calls=%fused_computation.37 | loop fusion | flops 657920 | bytes 2631680 | tf_op jit(solution)/shard_map/concatenate | solution.py:21
  82.4 1.1 copy.33
  89.5 1.6 %fusion.223 = (f32[8]{0:T(128)S(1)}, f32[8,4,16,512]{3,2,1,0:T(8,128)}) fusion(f32[8,4,16,512]{3,2,1,0:T(8,128)S(1)} %copy-done, f32[8,4,16,513]{3,2,1,0:T(8,128)S(1)} %broadcast_select_fusion, f32[8,4,17,512]{3,2,1,0:T(8,128)S(1)} %bitcast_dynamic-update-slice_fusion, f32[8,5,16,512]{3,2,1,0:T(8,128)S(1)} %add_dynamic-update-slice_fusion, f32[]{:T(128)S(6)} %div.553), kind=kLoop, calls=%fused_computation.747 | loop fusion | flops 2097144 | bytes 8388644 | tf_op jit(solution)/shard_map/reduce_sum | solution.py:152
  91.3 40.9 %all-reduce = f32[256]{0:T(256)S(1)} all-reduce(f32[256]{0:T(256)S(1)} %dynamic-update-slice), channel_id=2, replica_groups=mesh['gx'=4,'gy'=4,'gz'=2] {'gx','gy','gz'}, use_global_device_ids=true, to_apply=%add | all-reduce | flops 256 | bytes 2048
  (74 shorter events, 13.1 us)
Async XLA Ops:
  1.8 1.7 %copy-start = (f32[8,4,16,512]{3,2,1,0:T(8,128)S(1)}, f32[8,4,16,512]{3,2,1,0:T(8,128)}, u32[]{:S(2)}) copy-start(f32[8,4,16,512]{3,2,1,0:T(8,128)} %param.3) | copy-start | bytes 3145732
  15.4 1.0 copy-start.4
  16.4 1.0 copy-start.5
  18.2 6.7 %copy-start.1 = (f32[10,4,16,512]{3,2,1,0:T(8,128)}, f32[10,4,16,512]{3,2,1,0:T(8,128)S(1)}, u32[]{:S(2)}) copy-start(f32[10,4,16,512]{3,2,1,0:T(8,128)S(1)} %get-tuple-element.291) | copy-start | bytes 3932164
  18.2 6.7 %copy-start.2 = (f32[10,4,16,512]{3,2,1,0:T(8,128)}, f32[10,4,16,512]{3,2,1,0:T(8,128)S(1)}, u32[]{:S(2)}) copy-start(f32[10,4,16,512]{3,2,1,0:T(8,128)S(1)} %get-tuple-element.290) | copy-start | bytes 3932164
  19.1 67.7 %collective-permute-start = (f32[10,1,16,512]{3,2,1,0:T(8,128)}, f32[10,1,16,512]{3,2,1,0:T(8,128)S(1)}, u32[]{:S(2)}, u32[]{:S(2)}) collective-permute-start(f32[10,1,16,512]{3,2,1,0:T(8,128)} %get-tuple-element.277), channel_id=1, source_target_pairs={{0,8},{8,16},{16,24},{24,0},{1,9},{9,17},{17,25},{25,1},{2,10},{10... | collective-permute-start | bytes 983048 | tf_op jit(solution)/shard_map/ppermute | solution.py:19
  19.1 67.7 %collective-permute-start.1 = (f32[10,1,16,512]{3,2,1,0:T(8,128)}, f32[10,1,16,512]{3,2,1,0:T(8,128)S(1)}, u32[]{:S(2)}, u32[]{:S(2)}) collective-permute-start(f32[10,1,16,512]{3,2,1,0:T(8,128)} %get-tuple-element.278), channel_id=1, source_target_pairs={{8,0},{16,8},{24,16},{0,24},{9,1},{17,9},{25,17},{1,25},{10,2},{18... | collective-permute-start | bytes 983048 | tf_op jit(solution)/shard_map/ppermute | solution.py:20
  22.3 60.0 %collective-permute-start.2 = (f32[10,4,1,512]{3,0,2,1:T(8,128)}, f32[10,4,1,512]{3,0,2,1:T(8,128)}, u32[]{:S(2)}, u32[]{:S(2)}) collective-permute-start(f32[10,4,1,512]{3,0,2,1:T(8,128)} %copy.31), channel_id=1, source_target_pairs={{0,2},{2,4},{4,6},{6,0},{1,3},{3,5},{5,7},{7,1},{8,10},{10,12},{12... | collective-permute-start | bytes 245768 | tf_op jit(solution)/shard_map/ppermute | solution.py:19
  24.9 51.0 %collective-permute-start.4 = (f32[10,4,16,1]{3,2,1,0:T(8,128)}, f32[10,4,16,1]{3,2,1,0:T(8,128)}, u32[]{:S(2)}, u32[]{:S(2)}) collective-permute-start(f32[10,4,16,1]{3,2,1,0:T(8,128)} %get-tuple-element.281), channel_id=1, source_target_pairs={{0,1},{2,3},{4,5},{6,7},{8,9},{10,11},{12,13},{14,15},{16,17},{18,... | collective-permute-start | bytes 7688 | tf_op jit(solution)/shard_map/ppermute | solution.py:19
  26.1 51.6 %collective-permute-start.5 = (f32[10,4,16,1]{3,2,1,0:T(8,128)}, f32[10,4,16,1]{3,2,1,0:T(8,128)}, u32[]{:S(2)}, u32[]{:S(2)}) collective-permute-start(f32[10,4,16,1]{3,2,1,0:T(8,128)} %get-tuple-element.282), channel_id=1, source_target_pairs={{1,0},{3,2},{5,4},{7,6},{9,8},{11,10},{13,12},{15,14},{17,16},{19,... | collective-permute-start | bytes 7688 | tf_op jit(solution)/shard_map/ppermute | solution.py:20
  75.9 7.6 %collective-permute-start.3 = (f32[10,4,1,512]{3,0,2,1:T(8,128)S(1)}, f32[10,4,1,512]{3,0,2,1:T(8,128)S(1)}, u32[]{:S(2)}, u32[]{:S(2)}) collective-permute-start(f32[10,4,1,512]{3,0,2,1:T(8,128)S(1)} %copy.32), channel_id=1, source_target_pairs={{2,0},{4,2},{6,4},{0,6},{3,1},{5,3},{7,5},{1,7},{10,8},{12,10},{14... | collective-permute-start | bytes 245768 | tf_op jit(solution)/shard_map/ppermute | solution.py:20
  82.2 1.4 %copy-start.3 = (f32[10,4,16,512]{3,2,1,0:T(8,128)S(1)}, f32[10,4,16,512]{3,2,1,0:T(8,128)}, u32[]{:S(2)}) copy-start(f32[10,4,16,512]{3,2,1,0:T(8,128)} %copy-done.2) | copy-start | bytes 3932164
